TPU v7x, 8 devices: a whole 2x2x1 slice. The times are simulated.
8 devices in a mesh: dp: 1 (over z), ep: 8 (over y, x, core).
Axes of the slice: x: 2, y: 2, z: 1, core: 2. Of those that a mesh axis runs over, the one named last changes fastest.
Arguments:
- hidden: bfloat16 [2048, 1536], P(('dp', 'ep'))
- router_w: float32 [1536, 32], replicated
- expert_ids: int32 [2048, 2], P(('dp', 'ep'))
- w_gate: bfloat16 [32, 1536, 2304], P('ep')
- w_up: bfloat16 [32, 1536, 2304], P('ep')
- w_down: bfloat16 [32, 2304, 1536], P('ep')
- post_scale: float32 [2], replicated
Outputs:
- output: bfloat16 [2048, 1536], P(('dp', 'ep'))
All inputs are finite; a program needn't handle non-finite values.
Results may differ from a plain program's by a relative error of at most 0.001.
Values are sent between devices in bfloat16 or wider.
A program may use at most 1 GiB of HBM per device.

v0:
```python
import jax
import jax.numpy as jnp
from jax import lax
from jax.sharding import PartitionSpec as P


def route_tables(hidden, router_w, expert_ids, experts, capacity):
    tokens, choice_count = expert_ids.shape
    logits = jnp.dot(hidden.astype(jnp.float32), router_w, precision=lax.Precision.HIGHEST, preferred_element_type=jnp.float32)
    router_prob = jax.nn.softmax(logits, axis=-1)
    pick_mask = expert_ids[:, :, None] == jnp.arange(experts, dtype=jnp.int32)[None, None, :]
    picked = jnp.sum(jnp.where(pick_mask, router_prob[:, None, :], 0.0), axis=-1)
    gates = picked / jnp.sum(picked, axis=1, keepdims=True)
    pair_hot = pick_mask.reshape(tokens * choice_count, experts).astype(jnp.int32)
    earlier = jnp.cumsum(pair_hot, axis=0) - pair_hot
    slot_of = jnp.sum(earlier * pair_hot, axis=1).reshape(tokens, choice_count)
    slot_mask = slot_of[:, :, None] == jnp.arange(capacity, dtype=jnp.int32)[None, None, :]
    place = pick_mask[:, :, :, None] & slot_mask[:, :, None, :]
    return gates, place


def solution(mesh):
    ep_size = mesh.shape['ep']

    def local_step(hidden, router_w, expert_ids, w_gate, w_up, w_down, post_scale):
        tokens, model_width = hidden.shape
        local_experts = w_gate.shape[0]
        experts = local_experts * ep_size
        capacity = tokens // max(1, experts // 8)
        gates, place = route_tables(hidden, router_w, expert_ids, experts, capacity)
        token_table = jnp.any(place, axis=1).astype(jnp.bfloat16)
        outgoing = jnp.einsum('tec,td->ecd', token_table, hidden, preferred_element_type=jnp.float32).astype(jnp.bfloat16)
        incoming = lax.all_to_all(outgoing, 'ep', 0, 0, tiled=True).reshape(ep_size, local_experts, capacity, model_width)
        gate_in = jnp.einsum('slcd,ldf->slcf', incoming, w_gate, preferred_element_type=jnp.float32)
        up_in = jnp.einsum('slcd,ldf->slcf', incoming, w_up, preferred_element_type=jnp.float32)
        middle = (jax.nn.silu(gate_in) * up_in).astype(jnp.bfloat16)
        expert_out = jnp.einsum('slcf,lfd->slcd', middle, w_down, preferred_element_type=jnp.float32).astype(jnp.bfloat16)
        returned = lax.all_to_all(expert_out.reshape(experts, capacity, model_width), 'ep', 0, 0, tiled=True)
        pair_out = jnp.einsum('tkec,ecd->tkd', place.astype(jnp.bfloat16), returned, preferred_element_type=jnp.float32)
        mixed = jnp.sum(gates[:, :, None] * pair_out, axis=1)
        result = post_scale[0] * hidden.astype(jnp.float32) + post_scale[1] * mixed
        return result.astype(jnp.bfloat16)

    tok_spec = P(('dp', 'ep'))
    return jax.shard_map(local_step, mesh=mesh, in_specs=(tok_spec, P(), tok_spec, P('ep'), P('ep'), P('ep'), P()), out_specs=tok_spec, check_vma=False)
```

profile of v0, /device:TPU:0, one launch (start us, length us, event | category | flops | bytes accessed | tf_op | source)
XLA Modules:
  0.0 252.6 jit_solution(15804936667514713851)
XLA Ops:
  0.0 0.0 copy-start
  0.0 0.8 copy.9
  0.9 0.1 eq.58
  1.0 0.1 eq.62
  1.1 0.7 iota_compare_fusion.3
  1.9 1.2 reduce-window.6
  3.0 0.2 slice_reduce_fusion
  3.3 0.1 fusion.39
  3.4 0.1 eq.66
  3.6 0.1 copy.12
  3.7 0.5 and_reduce_fusion
  4.2 2.9 %convolution_convert_fusion = bf16[32,64,1536]{2,1,0:T(8,128)(2,1)S(1)} fusion(pred[256,32,64]{0,2,1:T(8,128)(4,1)S(1)} %and_reduce_fusion, bf16[256,1536]{1,0:T(8,128)(2,1)} %param.7), kind=kOutput, calls=%fused_computation.18 | convolution fusion | flops 1613758464 | bytes 7602176 | tf_op jit(solution)/shard_map/tec,td->ecd/dot_general | solution.py:32
  7.1 75.6 %all_to_all.10 = bf16[32,64,1536]{2,1,0:T(8,128)(2,1)} all-to-all(bf16[32,64,1536]{2,1,0:T(8,128)(2,1)S(1)} %convolution_convert_fusion), channel_id=1, replica_groups=mesh['dp'=1,'ep'=8] {'ep'}, dimensions={0} | all-to-all | bytes 12582912 | tf_op jit(solution)/shard_map/all_to_all | solution.py:33
  82.7 24.5 %fusion.2 = f32[4,8,64,2304]{3,2,1,0:T(8,128)} fusion(bf16[4,1536,2304]{2,1,0:T(8,128)(2,1)} %param.11, bf16[8,4,64,1536]{3,2,1,0:T(8,128)(2,1)} %bitcast.85), kind=kOutput, calls=%fused_computation.2 | convolution fusion | flops 14495514624 | bytes 53477376 | tf_op jit(solution)/shard_map/slcd,ldf->slcf/dot_general | solution.py:35
  107.2 32.3 %fusion.6 = bf16[8,4,64,2304]{3,2,0,1:T(8,128)(2,1)} fusion(f32[4,8,64,2304]{3,2,1,0:T(8,128)} %fusion.2, bf16[4,1536,2304]{2,1,0:T(8,128)(2,1)} %param.10, bf16[8,4,64,1536]{3,2,1,0:T(8,128)(2,1)} %bitcast.86), kind=kOutput, calls=%fused_computation.7 | convolution fusion | flops 14523826176 | bytes 62914560 | tf_op jit(solution)/shard_map/slcd,ldf->slcf/dot_general | solution.py:34
  139.5 23.1 %convert_bitcast_fusion = bf16[8,4,64,1536]{3,2,0,1:T(8,128)(2,1)} fusion(bf16[8,4,64,2304]{3,2,0,1:T(8,128)(2,1)} %fusion.6, bf16[4,2304,1536]{2,1,0:T(8,128)(2,1)} %param.12), kind=kOutput, calls=%fused_computation.15 | convolution fusion | flops 14498660352 | bytes 44040192 | tf_op jit(solution)/shard_map/slcf,lfd->slcd/dot_general | solution.py:37
  162.5 6.1 %copy.14 = bf16[8,4,64,1536]{3,2,1,0:T(8,128)(2,1)} copy(bf16[8,4,64,1536]{3,2,0,1:T(8,128)(2,1)} %convert_bitcast_fusion) | data formatting | bytes 12582912 | tf_op jit(solution)/shard_map/convert_element_type | solution.py:37
  168.6 0.0 copy-start.3
  168.6 0.0 copy-start.1
  168.6 0.0 copy-start.2
  168.6 3.8 %all-to-all-start.1 = ((bf16[32,64,1536]{2,1,0:T(8,128)(2,1)}), bf16[32,64,1536]{2,1,0:T(8,128)(2,1)}, u32[]{:S(2)}, u32[]{:S(2)}) async-start(bf16[32,64,1536]{2,1,0:T(8,128)(2,1)} %bitcast.84), calls=%async_computation.1 | async-start | bytes 12582912 | tf_op jit(solution)/shard_map/all_to_all | solution.py:38
  172.5 0.0 copy-done.3
  172.5 0.6 fusion.43
  173.1 0.0 copy-done
  173.1 0.0 copy-done.1
  173.1 0.8 fusion.44
  174.0 0.0 copy-done.2
  174.1 69.7 %all-to-all-done.1 = bf16[32,64,1536]{2,1,0:T(8,128)(2,1)} async-done(((bf16[32,64,1536]{2,1,0:T(8,128)(2,1)}), bf16[32,64,1536]{2,1,0:T(8,128)(2,1)}, u32[]{:S(2)}, u32[]{:S(2)}) %all-to-all-start.1) | async-done | bytes 6291488 | tf_op jit(solution)/shard_map/all_to_all | solution.py:38
  243.8 6.5 %fusion.31 = f32[256,1536]{1,0:T(8,128)S(1)} fusion(bf16[32,64,1536]{2,1,0:T(8,128)(2,1)} %all-to-all-done.1, pred[256,2,64]{0,2,1:T(8,128)(4,1)S(1)} %iota_compare_fusion, pred[256,2,32]{0,2,1:T(8,128)(4,1)S(1)} %iota_compare_fusion.3, f32[256,2]{0,1:T(2,128)S(1)} %broadcast_divide_fusion), kind=kOutput, calls=%fused_computation.25 | convolution fusion | flops 3223453696 | bytes 7915520 | tf_op jit(solution)/shard_map/tkec,ecd->tkd/dot_general | solution.py:39
  250.2 2.4 add_convert_fusion
  (8 shorter events, 0.2 us)
Async XLA Ops:
  0.0 173.1 %copy-start = (f32[1536,32]{0,1:T(8,128)S(1)}, f32[1536,32]{0,1:T(8,128)}, u32[]{:S(2)}) copy-start(f32[1536,32]{0,1:T(8,128)} %param.8) | copy-start | bytes 589828
  168.6 3.9 %copy-start.3 = (f32[2]{0:T(128)S(1)}, f32[2]{0:T(128)}, u32[]{:S(2)}) copy-start(f32[2]{0:T(128)} %param.13) | copy-start | bytes 28
  168.6 4.5 %copy-start.1 = (bf16[256,1536]{1,0:T(8,128)(2,1)S(1)}, bf16[256,1536]{1,0:T(8,128)(2,1)}, u32[]{:S(2)}) copy-start(bf16[256,1536]{1,0:T(8,128)(2,1)} %param.7) | copy-start | bytes 2359300
  168.6 5.4 %copy-start.2 = (s32[256,2]{0,1:T(2,128)S(1)}, s32[256,2]{0,1:T(2,128)}, u32[]{:S(2)}) copy-start(s32[256,2]{0,1:T(2,128)} %param.9) | copy-start | bytes 6148
  168.6 75.1 %all-to-all-start.1 = ((bf16[32,64,1536]{2,1,0:T(8,128)(2,1)}), bf16[32,64,1536]{2,1,0:T(8,128)(2,1)}, u32[]{:S(2)}, u32[]{:S(2)}) async-start(bf16[32,64,1536]{2,1,0:T(8,128)(2,1)} %bitcast.84), calls=%async_computation.1 | async-start | bytes 12582912 | tf_op jit(solution)/shard_map/all_to_all | solution.py:38
where the time goes:
time: 253 us
  matrix products  90 us (36%)
  blocking collectives  75.6 us (30%)
  waiting for transfers between devices  69.7 us (28%)
  local copies, waits for them, and re-layouts  8.34 us (3%)
  other arithmetic  5.07 us (2%)
  starting transfers between devices  3.84 us (2%)
    all_to_all x1, blocking collectives, local_step(): lax.all_to_all(outgoing, 'ep', 0, 0, tiled=True)  75.6 us
    all_to_all x1, waiting for transfers between devices, local_step(): lax.all_to_all(expert_out.reshape(experts, capacity, model_width), 'ep',...  69.7 us
    dot_general x1, matrix products, local_step(): jnp.einsum('slcd,ldf->slcf', incoming, w_gate, preferred_element_type=jnp...  32.3 us
    dot_general x1, matrix products, local_step(): jnp.einsum('slcd,ldf->slcf', incoming, w_up, preferred_element_type=jnp.f...  24.5 us
    dot_general x1, matrix products, local_step(): jnp.einsum('slcf,lfd->slcd', middle, w_down, preferred_element_type=jnp.f...  23.1 us
    dot_general x1, matrix products, local_step(): jnp.einsum('tkec,ecd->tkd', place.astype(jnp.bfloat16), returned, preferr...  6.46 us
    convert_element_type x1, local copies, waits for them, and re-layouts, local_step(): jnp.einsum('slcf,lfd->slcd', middle, w_down, preferred_element_type=jnp.f...  6.1 us
  transfers between devices with their start and end apart: 1, of which 1 were waited for; matrix products, arithmetic and copies ran while one was open for 1% of the time, Pallas kernels for 0%

commit v1 on v0

v1 whole, which is shorter than its diff:
```python
import functools

import jax
import jax.numpy as jnp
from jax import lax
from jax.experimental import pallas as pl
from jax.experimental.pallas import tpu as pltpu
from jax.sharding import PartitionSpec as P

MESH = pl.DeviceIdType.MESH
F32, BF16, I32 = jnp.float32, jnp.bfloat16, jnp.int32
NT = (((1,), (1,)), ((), ()))


def flip(idx, mask):
    out = idx
    for bit in (1, 2, 4):
        if mask & bit:
            out = out + bit - 2 * bit * ((idx // bit) % 2)
    return out


def dev(idx):
    return (lax.axis_index('dp'), idx)


def iota(shape, dim):
    return lax.broadcasted_iota(I32, shape, dim)


CHUNKS = 4


def gather_kernel(caps, hid, ids, wrt, h_all, pos, tok, cap, ids_all, send, recv, id_send, id_recv, own_sem):
    me = lax.axis_index('ep')
    tokens, width = hid.shape
    experts = wrt.shape[0]
    owners = h_all.shape[0]
    local = experts // owners
    rows = tokens // CHUNKS
    barrier = pltpu.get_barrier_semaphore()
    for q in range(1, owners):
        pl.semaphore_signal(barrier, inc=1, device_id=dev(flip(me, q)), device_id_type=MESH)
    pl.semaphore_wait(barrier, owners - 1)

    def piece(ref, c):
        return ref.at[pl.ds(c * rows, rows)]

    def remote(src, dst, n, to):
        return pltpu.make_async_remote_copy(src_ref=src, dst_ref=dst, send_sem=send.at[n], recv_sem=recv.at[n], device_id=dev(to), device_id_type=MESH)

    xn, yn, dg, mate = flip(me, 2), flip(me, 4), flip(me, 6), flip(me, 1)
    id_copies = []
    for q in range(1, owners):
        id_copies.append(pltpu.make_async_remote_copy(src_ref=ids, dst_ref=ids_all.at[q], send_sem=id_send.at[q], recv_sem=id_recv.at[q], device_id=dev(flip(me, q)), device_id_type=MESH))
    for c in id_copies:
        c.start()
    x_order, y_order = (0, 1, 2, 3), (2, 3, 0, 1)
    to_x = {c: remote(piece(hid, c), piece(h_all.at[me], c), c, xn) for c in x_order}
    to_y = {c: remote(piece(hid, c), piece(h_all.at[me], c), 4 + c, yn) for c in y_order}
    for cx, cy in zip(x_order, y_order):
        to_x[cx].start()
        to_y[cy].start()
    to_mate = remote(hid, h_all.at[me], 24, mate)
    to_mate.start()
    own = pltpu.make_async_copy(hid, h_all.at[me], own_sem)
    own.start()

    h = hid[...]
    w = wrt[...]
    w_hi = w.astype(BF16)
    rest = w - w_hi.astype(F32)
    w_mid = rest.astype(BF16)
    w_lo = (rest - w_mid.astype(F32)).astype(BF16)
    dot = functools.partial(lax.dot_general, dimension_numbers=NT, preferred_element_type=F32)
    logits = dot(h, w_hi) + (dot(h, w_mid) + dot(h, w_lo))
    ex = jnp.exp(logits - jnp.max(logits, axis=1, keepdims=True))
    prob = ex / jnp.sum(ex, axis=1, keepdims=True)
    eye = (iota((tokens, tokens), 0) == iota((tokens, tokens), 1)).astype(F32).astype(BF16)
    own_ids = ids[...].astype(F32)
    lane = iota((tokens, experts), 1).astype(F32)
    id_col = [dot(eye, jnp.broadcast_to(own_ids[k:k + 1], (8, tokens)).astype(BF16))[:, 0:1] for k in (0, 1)]
    pick = [(id_col[k] == lane).astype(F32) for k in (0, 1)]
    g = [jnp.sum(pick[k] * prob, axis=1, keepdims=True) for k in (0, 1)]
    total = g[0] + g[1]

    for c in id_copies:
        c.wait_recv()
    ids_all[0] = ids[...]
    most = None
    for q in range(owners):
        both = ids_all[q]
        e_col = iota((experts, tokens), 0)
        hot = ((both[0:1] == e_col) | (both[1:2] == e_col)).astype(F32).astype(BF16)
        count = dot(jnp.ones((8, tokens), BF16), hot)
        most = count if most is None else jnp.maximum(most, count)
    stride = jnp.floor((most + 15.0) * (1.0 / 16.0)) * 16.0
    ea, eb = iota((experts, experts), 0), iota((experts, experts), 1)
    same = ea // local == eb // local
    plain = functools.partial(jnp.dot, preferred_element_type=F32)
    offset = plain(stride.astype(BF16), (same & (ea < eb)).astype(F32).astype(BF16))
    need = jnp.max(plain(stride.astype(BF16), same.astype(F32).astype(BF16))).astype(I32)
    branch = jnp.int32(0)
    for limit in caps[:-1]:
        branch = branch + (need > limit).astype(I32)
    cap[0] = branch
    ta, tb = iota((tokens, tokens), 0), iota((tokens, tokens), 1)
    before = (tb < ta).astype(F32).astype(BF16)
    rank = plain(before, (pick[0] + pick[1]).astype(BF16))
    place = rank + offset[0:1]
    slot = [jnp.sum(pick[k] * place, axis=1, keepdims=True) for k in (0, 1)]
    owner = [jnp.floor(id_col[k] * (1.0 / local)) for k in (0, 1)]
    wide = iota((tokens, 128), 1)
    table = jnp.zeros((tokens, 128), F32)
    for n, col in enumerate((g[0] / total, g[1] / total, owner[0], owner[1], slot[0], slot[1])):
        table = jnp.where(wide == n, col, table)
    tok[...] = table
    rows_of = [[], []]
    for s in range(owners):
        both = ids_all[flip(me, s)]
        for k in (0, 1):
            rows_of[k].append(both[k:k + 1])
    first, second = (jnp.concatenate(rows_of[k], axis=0) for k in (0, 1))
    marks = jnp.concatenate([((first == me * local + j) | (second == me * local + j)).astype(F32) for j in range(local)], axis=0)
    earlier = plain(marks.astype(BF16), (ta < tb).astype(F32).astype(BF16))
    pos[...] = jnp.where(marks > 0.5, earlier, -1.0)

    sent = [*to_x.values(), *to_y.values(), to_mate]
    relayed = []
    for cx, cy in zip(x_order, y_order):
        to_x[cx].wait_recv()
        if cx in (0, 1):
            f = remote(piece(h_all.at[xn], cx), piece(h_all.at[xn], cx), 8 + cx, yn)
            f.start()
            relayed.append((cx, f))
        m = remote(piece(h_all.at[xn], cx), piece(h_all.at[xn], cx), 12 + cx, mate)
        m.start()
        sent.append(m)
        to_y[cy].wait_recv()
        if cy in (2, 3):
            f = remote(piece(h_all.at[yn], cy), piece(h_all.at[yn], cy), 8 + cy, xn)
            f.start()
            relayed.append((cy, f))
        m = remote(piece(h_all.at[yn], cy), piece(h_all.at[yn], cy), 16 + cy, mate)
        m.start()
        sent.append(m)
    for c, f in relayed:
        f.wait_recv()
        m = remote(piece(h_all.at[dg], c), piece(h_all.at[dg], c), 20 + c, mate)
        m.start()
        sent.append(m)
        sent.append(f)
    to_mate.wait_recv()
    for m in sent[9:]:
        if not any(m is f for _, f in relayed):
            m.wait_recv()
    for m in sent:
        m.wait_send()
    for c in id_copies:
        c.wait_send()
    own.wait()


def gather_call(hidden, ids_t, wr_t, owners, caps):
    tokens, width = hidden.shape
    experts = wr_t.shape[0]
    vmem = pl.BlockSpec(memory_space=pltpu.VMEM)
    return pl.pallas_call(
        functools.partial(gather_kernel, caps),
        name='gather_tokens',
        out_shape=(
            jax.ShapeDtypeStruct((owners, tokens, width), BF16),
            jax.ShapeDtypeStruct((experts // owners * owners, tokens), F32),
            jax.ShapeDtypeStruct((tokens, 128), F32),
            jax.ShapeDtypeStruct((1,), I32),
        ),
        in_specs=[vmem, vmem, vmem],
        out_specs=(pl.BlockSpec(memory_space=pl.ANY), vmem, vmem, pl.BlockSpec(memory_space=pltpu.SMEM)),
        scratch_shapes=[
            pltpu.VMEM((owners, 2, tokens), I32),
            pltpu.SemaphoreType.DMA((25,)),
            pltpu.SemaphoreType.DMA((25,)),
            pltpu.SemaphoreType.DMA((owners,)),
            pltpu.SemaphoreType.DMA((owners,)),
            pltpu.SemaphoreType.DMA,
        ],
        compiler_params=pltpu.CompilerParams(collective_id=0, has_side_effects=True),
    )(hidden, ids_t, wr_t)


NF = 3
RING = 4


def expert_kernel(caps, branch, pos, h_all, w1, w3, w2, ret, hbuf, xbuf, w1b, w3b, w2b, hot, mid, yacc, ybuf, zero, plan, hsem, wsem, ysem, zsem):
    sources, tokens, width = h_all.shape
    local, _, ffn = w1.shape
    ft = ffn // NF
    steps = local * NF
    slots = hot.shape[0] // local

    unit = []
    for j in range(local):
        most = jnp.max(pos[pl.ds(j * sources, sources), :]).astype(I32) + 1
        unit.append((most + 15) // 16)
    for j in range(local):
        rank = jnp.int32(0)
        offset = jnp.int32(0)
        for i in range(local):
            if i != j:
                ahead = (unit[i] >= unit[j]) if i < j else (unit[i] > unit[j])
                rank = rank + ahead.astype(I32)
            if i < j:
                offset = offset + unit[i]
        plan[0, rank] = jnp.int32(j)
        plan[1, rank] = unit[j]
        plan[2, rank] = offset
    used = unit[0] + unit[1] + unit[2] + unit[3]

    def weights(t):
        e = plan[0, t // NF]
        cols = pl.ds(pl.multiple_of((t % NF) * ft, ft), ft)
        n = t % RING
        return (
            pltpu.make_async_copy(w1.at[e, :, cols], w1b.at[n], wsem.at[n, 0]),
            pltpu.make_async_copy(w3.at[e, :, cols], w3b.at[n], wsem.at[n, 1]),
            pltpu.make_async_copy(w2.at[e, cols, :], w2b.at[n], wsem.at[n, 2]),
        )

    def tokens_in(s):
        return pltpu.make_async_copy(h_all.at[s], hbuf.at[s], hsem.at[s])

    for s in range(sources):
        tokens_in(s).start()
    for t in range(RING):
        for c in weights(jnp.int32(t)):
            c.start()

    limit = jnp.int32(caps[0])
    for n in range(1, len(caps)):
        limit = jnp.where(branch[0] >= n, caps[n], limit)
    zero[...] = jnp.zeros_like(zero)
    spare = limit // 16 - used

    def fill(n):
        s, u = n // spare, n % spare
        return pltpu.make_async_copy(zero, ret.at[s, pl.ds(pl.multiple_of((used + u) * 16, 16), 16)], zsem)

    for s in range(sources):
        tokens_in(s).wait()
        for r in range(local):
            row = pos[pl.ds(plan[0, r] * sources + s, 1), :]
            match = iota((slots, tokens), 0).astype(F32) == row
            hot[pl.ds(r * slots, slots), :] = match.astype(F32).astype(BF16)

        @pl.loop(0, width // 512)
        def _(n):
            cols = pl.ds(pl.multiple_of(n * 512, 512), 512)
            part = jnp.dot(hot[...], hbuf[s, :, cols], preferred_element_type=F32).astype(BF16)
            for r in range(local):
                first = pl.multiple_of(plan[1, r] * (16 * s), 16)
                xbuf[r, pl.ds(first, slots), cols] = part[r * slots:(r + 1) * slots]

    @pl.loop(0, sources * spare)
    def _(n):
        fill(n).start()

    def out_copies(r, units):
        st = 16 * units
        first = pl.multiple_of(plan[2, r] * 16, 16)
        return [pltpu.make_async_copy(ybuf.at[r, pl.ds(s * st, st)], ret.at[s, pl.ds(first, st)], ysem) for s in range(sources)]

    @pl.loop(0, local)
    def _(r):
        @pl.loop(0, NF)
        def _(f):
            t = r * NF + f
            n = t % RING
            for c in weights(t):
                c.wait()
            for units in range(1, slots // 16 + 1):
                m = 16 * units * sources

                @pl.when(plan[1, r] == units)
                def _():
                    @pl.loop(0, ft // 256)
                    def _(i):
                        cols = pl.ds(pl.multiple_of(i * 256, 256), 256)
                        gate = jnp.dot(xbuf[r, 0:m, :], w1b[n, :, cols], preferred_element_type=F32)
                        up = jnp.dot(xbuf[r, 0:m, :], w3b[n, :, cols], preferred_element_type=F32)
                        mid[0:m, cols] = (gate * jax.nn.sigmoid(gate) * up).astype(BF16)

                    @pl.loop(0, width // 512)
                    def _(i):
                        cols = pl.ds(pl.multiple_of(i * 512, 512), 512)
                        part = jnp.dot(mid[0:m, :], w2b[n, :, cols], preferred_element_type=F32)
                        old = yacc[0:m, cols]
                        yacc[0:m, cols] = jnp.where(f == 0, 0.0, old) + part

                    @pl.when(f == NF - 1)
                    def _():
                        ybuf[r, 0:m, :] = yacc[0:m, :].astype(BF16)
                        for c in out_copies(r, units):
                            c.start()

            @pl.when(t + RING < steps)
            def _():
                for c in weights(t + RING):
                    c.start()

    @pl.loop(0, local)
    def _(r):
        for units in range(1, slots // 16 + 1):
            @pl.when(plan[1, r] == units)
            def _():
                for c in out_copies(r, units):
                    c.wait()

    @pl.loop(0, sources * spare)
    def _(n):
        fill(n).wait()


def expert_call(branch, pos, h_all, w1, w3, w2, caps):
    sources, tokens, width = h_all.shape
    local, _, ffn = w1.shape
    slots = caps[-1] // local
    ft = ffn // NF
    hbm = pl.BlockSpec(memory_space=pl.ANY)
    flops = 3 * 2 * local * slots * sources * width * ffn // 2
    return pl.pallas_call(
        functools.partial(expert_kernel, caps),
        name='experts',
        out_shape=jax.ShapeDtypeStruct((sources, caps[-1], width), BF16),
        in_specs=[pl.BlockSpec(memory_space=pltpu.SMEM), pl.BlockSpec(memory_space=pltpu.VMEM), hbm, hbm, hbm, hbm],
        out_specs=hbm,
        scratch_shapes=[
            pltpu.VMEM((sources, tokens, width), BF16),
            pltpu.VMEM((local, sources * slots + slots, width), BF16),
            pltpu.VMEM((RING, width, ft), BF16),
            pltpu.VMEM((RING, width, ft), BF16),
            pltpu.VMEM((RING, ft, width), BF16),
            pltpu.VMEM((local * slots, tokens), BF16),
            pltpu.VMEM((sources * slots, ft), BF16),
            pltpu.VMEM((sources * slots, width), F32),
            pltpu.VMEM((local, sources * slots, width), BF16),
            pltpu.VMEM((16, width), BF16),
            pltpu.SMEM((3, local), I32),
            pltpu.SemaphoreType.DMA((sources,)),
            pltpu.SemaphoreType.DMA((RING, 3)),
            pltpu.SemaphoreType.DMA,
            pltpu.SemaphoreType.DMA,
        ],
        compiler_params=pltpu.CompilerParams(vmem_limit_bytes=60 * 1024 * 1024),
        cost_estimate=pl.CostEstimate(flops=flops, bytes_accessed=3 * 2 * local * width * ffn, transcendentals=0),
    )(branch, pos, h_all, w1, w3, w2)


ORDER = (0, 1, 2, 4, 6, 3, 5, 7)


def return_kernel(cap, ret, tok, hid, scale, out, got, acc, send, recv):
    me = lax.axis_index('ep')
    owners = ret.shape[0]
    tokens, width = hid.shape
    barrier = pltpu.get_barrier_semaphore()
    for q in range(1, owners):
        pl.semaphore_signal(barrier, inc=1, device_id=dev(flip(me, q)), device_id_type=MESH)
    pl.semaphore_wait(barrier, owners - 1)
    copies = {}
    for q in ORDER[2:] + (1,):
        to = flip(me, q)
        copies[q] = pltpu.make_async_remote_copy(src_ref=ret.at[to, pl.ds(0, cap)], dst_ref=got.at[q], send_sem=send.at[q], recv_sem=recv.at[q], device_id=dev(to), device_id_type=MESH)
        copies[q].start()
    own = pltpu.make_async_copy(ret.at[me, pl.ds(0, cap)], got.at[0], recv.at[0])
    own.start()
    table = tok[...]
    lane = iota((tokens, cap), 1).astype(F32)
    for q in ORDER:
        if q == 0:
            own.wait()
        else:
            copies[q].wait_recv()
        peer = flip(me, q).astype(F32)
        hot = jnp.concatenate([((table[:, 2 + k:3 + k] == peer) & (table[:, 4 + k:5 + k] == lane)).astype(F32).astype(BF16) for k in (0, 1)], axis=0)

        @pl.loop(0, width // 256)
        def _(n):
            cols = pl.ds(pl.multiple_of(n * 256, 256), 256)
            part = jnp.dot(hot, got[q, :, cols], preferred_element_type=F32)
            acc[:, cols] = part if q == 0 else acc[:, cols] + part

    mixed = table[:, 0:1] * acc[0:tokens] + table[:, 1:2] * acc[tokens:2 * tokens]
    out[...] = (scale[0] * hid[...].astype(F32) + scale[1] * mixed).astype(BF16)
    for q in copies:
        copies[q].wait_send()


def return_call(n, cap, ret, tok, hidden, scale):
    owners, _, width = ret.shape
    tokens = hidden.shape[0]
    vmem = pl.BlockSpec(memory_space=pltpu.VMEM)
    return pl.pallas_call(
        functools.partial(return_kernel, cap),
        name=f'return_{cap}',
        out_shape=jax.ShapeDtypeStruct((tokens, width), BF16),
        in_specs=[pl.BlockSpec(memory_space=pl.ANY), vmem, vmem, pl.BlockSpec(memory_space=pltpu.SMEM)],
        out_specs=vmem,
        scratch_shapes=[
            pltpu.VMEM((owners, cap, width), BF16),
            pltpu.VMEM((2 * tokens, width), F32),
            pltpu.SemaphoreType.DMA((owners,)),
            pltpu.SemaphoreType.DMA((owners,)),
        ],
        compiler_params=pltpu.CompilerParams(collective_id=1 + n, has_side_effects=True, vmem_limit_bytes=40 * 1024 * 1024),
    )(ret, tok, hidden, scale)


def capacities(local, slots):
    full = [slots * n + 16 * (local - n) for n in range(1, local + 1)]
    return tuple(sorted({full[0] + 16, *full}))


def solution(mesh):
    owners = mesh.shape['ep']

    def local_step(hidden, router_w, expert_ids, w_gate, w_up, w_down, post_scale):
        tokens = hidden.shape[0]
        local = w_gate.shape[0]
        slots = tokens // max(1, local * owners // 8)
        caps = capacities(local, slots)
        h_all, pos, tok, branch = gather_call(hidden, expert_ids.T, router_w.T, owners, caps)
        ret = expert_call(branch, pos, h_all, w_gate, w_up, w_down, caps)
        branches = [functools.partial(return_call, n, cap) for n, cap in enumerate(caps)]
        return lax.switch(branch[0], branches, ret, tok, hidden, post_scale)

    tok_spec = P(('dp', 'ep'))
    return jax.shard_map(local_step, mesh=mesh, in_specs=(tok_spec, P(), tok_spec, P('ep'), P('ep'), P('ep'), P()), out_specs=tok_spec, check_vma=False)
```

time: 253 us -> 140 us (0.55)
  Pallas kernels: 0 us -> 138 us
  matrix products: 90 us -> 0 us
  blocking collectives: 75.6 us -> 0 us
  waiting for transfers between devices: 69.7 us -> 0 us
  local copies, waits for them, and re-layouts: 8.34 us -> 0.89 us
  other arithmetic: 5.07 us -> 0 us
  starting transfers between devices: 3.84 us -> 0 us
    pallas_call x0 -> x3, Pallas kernels: none -> 138 us  [the longest x1 63.3 us: return_call(): pl.pallas_call(functools.partial(return_kernel, cap), name=f'return_{cap}...]
    dot_general x6 -> x0, matrix products: 90 us -> none  [the longest x1 32.3 us: local_step(): jnp.einsum('slcd,ldf->slcf', incoming, w_gate, preferred_element_type=jnp...]
    all_to_all x1 -> x0, blocking collectives: 75.6 us -> none  [local_step(): lax.all_to_all(outgoing, 'ep', 0, 0, tiled=True)]
    all_to_all x1 -> x0, waiting for transfers between devices: 69.7 us -> none  [local_step(): lax.all_to_all(expert_out.reshape(experts, capacity, model_width), 'ep',...]
    convert_element_type x1 -> x0, local copies, waits for them, and re-layouts: 6.1 us -> none  [local_step(): jnp.einsum('slcf,lfd->slcd', middle, w_down, preferred_element_type=jnp.f...]
    all_to_all x1 -> x0, starting transfers between devices: 3.84 us -> none  [local_step(): lax.all_to_all(expert_out.reshape(experts, capacity, model_width), 'ep',...]
  transfers between devices with their start and end apart: 1 -> 0, of which waited for: 1 -> 0; matrix products, arithmetic and copies ran while one was open for 1% -> 0% of each run, Pallas kernels for 0% -> 0%
where the time goes in v1:
time: 140 us
  Pallas kernels  138 us (99%)
    pallas_call x1, Pallas kernels, return_call(): pl.pallas_call(functools.partial(return_kernel, cap), name=f'return_{cap}...  63.3 us
    pallas_call x1, Pallas kernels, expert_call(): pl.pallas_call(functools.partial(expert_kernel, caps), name='experts', ou...  39.4 us
    pallas_call x1, Pallas kernels, gather_call(): pl.pallas_call(functools.partial(gather_kernel, caps), name='gather_token...  35 us

profile of v1, /device:TPU:0, one launch (start us, length us, event | category | flops | bytes accessed | tf_op | source)
XLA Modules:
  0.0 139.7 jit_solution(325987595091938407)
XLA Ops:
  0.0 35.0 %gather_tokens.1 = (bf16[8,256,1536]{2,1,0:T(8,128)(2,1)}, f32[32,256]{1,0:T(8,128)}, f32[256,128]{1,0:T(8,128)S(1)}, s32[1]{0:T(128)}) custom-call(bf16[256,1536]{1,0:T(8,128)(2,1)} %hid.1, s32[2,256]{1,0:T(2,128)} %bitcast.4, f32[32,1536]{1,0:T(8,128)} %bitcast.3), custom_call_target="tpu_custom_call" | custom-call | tf_op jit(solution)/shard_map/gather_tokens/pallas_call | solution.py:168
  35.1 0.0 copy-start
  35.1 0.0 copy-start.1
  35.1 39.4 %experts.1 = bf16[8,256,1536]{2,1,0:T(8,128)(2,1)} custom-call(s32[1]{0:T(128)} %get-tuple-element.75.branch, f32[32,256]{1,0:T(8,128)} %get-tuple-element.76.pos, bf16[8,256,1536]{2,1,0:T(8,128)(2,1)} %get-tuple-element.77.h_all, bf16[4,1536,2304]{2,1,0:T(8,128)(2,1)} %w1.1, bf16[4,1536,2304]{2,1,0:T(8,128)(2,1)} %w3.1, bf16[4,2304,1536]{2,1,0:T(8,128)(2,1)} %w2.1), custom_call_target="tpu_custom_call" | custom-call | flops 21743271936 | bytes 84934656 | tf_op jit(solution)/shard_map/experts/pallas_call | solution.py:331
  75.1 0.0 copy-done
  75.1 0.0 copy-done.1
  75.1 63.7 %conditional.1 = (bf16[256,1536]{1,0:T(8,128)(2,1)S(1)}) conditional(s32[]{:T(128)} %bitcast.2, (bf16[8,256,1536]{2,1,0:T(8,128)(2,1)}, f32[256,128]{1,0:T(8,128)S(1)}, bf16[256,1536]{1,0:T(8,128)(2,1)S(1)}, f32[2]{0:T(128)S(1)}) %tuple.36, (bf16[8,256,1536]{2,1,0:T(8,128)(2,1)}, f32[256,128]{1,0:T(8,128)S(1)}, ...), branch_computations={%region_0.0_spmd, %region_1.0_spmd, %region_2.0_spmd, %region_3.0_... | conditional | bytes 8 | solution.py:435
  75.3 63.3 %return_160.1 = bf16[256,1536]{1,0:T(8,128)(2,1)S(1)} custom-call(bf16[8,256,1536]{2,1,0:T(8,128)(2,1)} %get-tuple-element.59.ret, f32[256,128]{1,0:T(8,128)S(1)} %get-tuple-element.60.tok, bf16[256,1536]{1,0:T(8,128)(2,1)S(1)} %get-tuple-element.61.hid, f32[2]{0:T(128)S(1)} %get-tuple-element.87.scale), custom_call_target="tpu_custom_call" | custom-call | tf_op jit(solution)/shard_map/cond/branch_2_fun/return_160/pallas_call | solution.py:403
  138.8 0.9 copy.24
Async XLA Ops:
  35.1 40.0 %copy-start = (bf16[256,1536]{1,0:T(8,128)(2,1)S(1)}, bf16[256,1536]{1,0:T(8,128)(2,1)}, u32[]{:S(2)}) copy-start(bf16[256,1536]{1,0:T(8,128)(2,1)} %hid.1) | copy-start | bytes 2359300
  35.1 40.0 %copy-start.1 = (f32[2]{0:T(128)S(1)}, f32[2]{0:T(128)}, u32[]{:S(2)}) copy-start(f32[2]{0:T(128)} %param.18) | copy-start | bytes 28

commit v2 on v1

v2 whole, which is shorter than its diff:
```python
import functools

import jax
import jax.numpy as jnp
from jax import lax
from jax.experimental import pallas as pl
from jax.experimental.pallas import tpu as pltpu
from jax.sharding import PartitionSpec as P

MESH = pl.DeviceIdType.MESH
F32, BF16, I32 = jnp.float32, jnp.bfloat16, jnp.int32
NT = (((1,), (1,)), ((), ()))


def flip(idx, mask):
    out = idx
    for bit in (1, 2, 4):
        if mask & bit:
            out = out + bit - 2 * bit * ((idx // bit) % 2)
    return out


def dev(idx):
    return (lax.axis_index('dp'), idx)


def iota(shape, dim):
    return lax.broadcasted_iota(I32, shape, dim)


CHUNKS = 4
NF = 3
RING = 2


def gather_kernel(caps, hid, ids, wrt, w1, w3, w2, rows_out, pos, tok, cap, w1p, w3p, w2p, land, ids_all, send, recv, id_send, id_recv, wsem):
    me = lax.axis_index('ep')
    tokens, width = hid.shape
    experts = wrt.shape[0]
    local, owners, slots, _ = rows_out.shape
    ft = w1p.shape[2]
    rows = tokens // CHUNKS
    barrier = pltpu.get_barrier_semaphore()
    for q in range(1, owners):
        pl.semaphore_signal(barrier, inc=1, device_id=dev(flip(me, q)), device_id_type=MESH)
    pl.semaphore_wait(barrier, owners - 1)

    def piece(q, c):
        return (hid if q == 0 else land.at[q]).at[pl.ds(c * rows, rows)]

    def remote(q, c, n, to):
        return pltpu.make_async_remote_copy(src_ref=piece(q, c), dst_ref=land.at[q ^ to, pl.ds(c * rows, rows)], send_sem=send.at[n], recv_sem=recv.at[n], device_id=dev(flip(me, to)), device_id_type=MESH)

    id_copies = []
    for q in range(1, owners):
        id_copies.append(pltpu.make_async_remote_copy(src_ref=ids, dst_ref=ids_all.at[q], send_sem=id_send.at[q], recv_sem=id_recv.at[q], device_id=dev(flip(me, q)), device_id_type=MESH))
    for c in id_copies:
        c.start()
    x_order, y_order = (0, 1, 2, 3), (2, 3, 0, 1)
    to_x = {c: remote(0, c, c, 2) for c in x_order}
    to_y = {c: remote(0, c, 4 + c, 4) for c in y_order}
    for cx, cy in zip(x_order, y_order):
        to_x[cx].start()
        to_y[cy].start()
    to_mate = pltpu.make_async_remote_copy(src_ref=hid, dst_ref=land.at[1], send_sem=send.at[24], recv_sem=recv.at[24], device_id=dev(flip(me, 1)), device_id_type=MESH)
    to_mate.start()
    early = []
    for f in range(NF):
        cols = pl.ds(f * ft, ft)
        early += [
            pltpu.make_async_copy(w1.at[0, :, cols], w1p.at[f], wsem.at[f, 0]),
            pltpu.make_async_copy(w3.at[0, :, cols], w3p.at[f], wsem.at[f, 1]),
            pltpu.make_async_copy(w2.at[0, cols, :], w2p.at[f], wsem.at[f, 2]),
        ]
    for c in early:
        c.start()

    h = hid[...]
    w = wrt[...]
    w_hi = w.astype(BF16)
    rest = w - w_hi.astype(F32)
    w_mid = rest.astype(BF16)
    w_lo = (rest - w_mid.astype(F32)).astype(BF16)
    dot = functools.partial(lax.dot_general, dimension_numbers=NT, preferred_element_type=F32)
    logits = dot(h, w_hi) + (dot(h, w_mid) + dot(h, w_lo))
    ex = jnp.exp(logits - jnp.max(logits, axis=1, keepdims=True))
    prob = ex / jnp.sum(ex, axis=1, keepdims=True)
    ta, tb = iota((tokens, tokens), 0), iota((tokens, tokens), 1)
    eye = (ta == tb).astype(F32).astype(BF16)
    own_ids = ids[...].astype(F32)
    lane = iota((tokens, experts), 1).astype(F32)
    id_col = [dot(eye, jnp.broadcast_to(own_ids[k:k + 1], (8, tokens)).astype(BF16))[:, 0:1] for k in (0, 1)]
    pick = [(id_col[k] == lane).astype(F32) for k in (0, 1)]
    g = [jnp.sum(pick[k] * prob, axis=1, keepdims=True) for k in (0, 1)]
    total = g[0] + g[1]

    for c in id_copies:
        c.wait_recv()
    ids_all[0] = ids[...]
    most = None
    for q in range(owners):
        both = ids_all[q]
        e_col = iota((experts, tokens), 0)
        hot = ((both[0:1] == e_col) | (both[1:2] == e_col)).astype(F32).astype(BF16)
        count = dot(jnp.ones((8, tokens), BF16), hot)
        most = count if most is None else jnp.maximum(most, count)
    stride = jnp.floor((most + 15.0) * (1.0 / 16.0)) * 16.0
    ea, eb = iota((experts, experts), 0), iota((experts, experts), 1)
    same = ea // local == eb // local
    plain = functools.partial(jnp.dot, preferred_element_type=F32)
    offset = plain(stride.astype(BF16), (same & (ea < eb)).astype(F32).astype(BF16))
    need = jnp.max(plain(stride.astype(BF16), same.astype(F32).astype(BF16))).astype(I32)
    branch = jnp.int32(0)
    for limit in caps[:-1]:
        branch = branch + (need > limit).astype(I32)
    cap[0] = branch
    rank = plain((tb < ta).astype(F32).astype(BF16), (pick[0] + pick[1]).astype(BF16))
    place = rank + offset[0:1]
    slot = [jnp.sum(pick[k] * place, axis=1, keepdims=True) for k in (0, 1)]
    owner = [jnp.floor(id_col[k] * (1.0 / local)) for k in (0, 1)]
    wide = iota((tokens, 128), 1)
    table = jnp.zeros((tokens, 128), F32)
    for n, col in enumerate((g[0] / total, g[1] / total, owner[0], owner[1], slot[0], slot[1])):
        table = jnp.where(wide == n, col, table)
    tok[...] = table
    first, second = (jnp.concatenate([ids_all[q, k:k + 1] for q in range(owners)], axis=0) for k in (0, 1))
    marks = jnp.concatenate([((first == me * local + j) | (second == me * local + j)).astype(F32) for j in range(local)], axis=0)
    earlier = plain(marks.astype(BF16), (ta < tb).astype(F32).astype(BF16))
    pos[...] = jnp.where(marks > 0.5, earlier, -1.0)

    def pick_rows(q):
        at = iota((slots, tokens), 0).astype(F32)
        match = jnp.concatenate([(at == pos[j * owners + q:j * owners + q + 1, :]).astype(F32) for j in range(local)], axis=0).astype(BF16)

        @pl.loop(0, width // 512)
        def _(n):
            cols = pl.ds(pl.multiple_of(n * 512, 512), 512)
            block = hid[:, cols] if q == 0 else land[q, :, cols]
            part = jnp.dot(match, block, preferred_element_type=F32).astype(BF16)
            for j in range(local):
                rows_out[j, q, :, cols] = part[j * slots:(j + 1) * slots]

    sent = [*to_x.values(), *to_y.values(), to_mate]

    def pass_on(q, c, n, to):
        copy = remote(q, c, n, to)
        copy.start()
        sent.append(copy)
        return copy

    pick_rows(0)
    across, mates = {}, {2: [], 4: [], 6: []}
    for cx, cy in zip(x_order, y_order):
        to_x[cx].wait_recv()
        if cx in (0, 1):
            across[cx] = pass_on(2, cx, 8 + cx, 4)
        mates[2].append(pass_on(2, cx, 12 + cx, 1))
        to_y[cy].wait_recv()
        if cy in (2, 3):
            across[cy] = pass_on(4, cy, 8 + cy, 2)
        mates[4].append(pass_on(4, cy, 16 + cy, 1))
        if cx == 0:
            to_mate.wait_recv()
            pick_rows(1)
    for q in (2, 4):
        pick_rows(q)
    for q in (2, 4):
        for m in mates[q]:
            m.wait_recv()
        pick_rows(q + 1)
    for c in (0, 2, 1, 3):
        across[c].wait_recv()
        mates[6].append(pass_on(6, c, 20 + c, 1))
    pick_rows(6)
    for m in mates[6]:
        m.wait_recv()
    pick_rows(7)
    for m in sent:
        m.wait_send()
    for c in id_copies:
        c.wait_send()
    for c in early:
        c.wait()


def gather_call(hidden, ids_t, wr_t, w1, w3, w2, owners, caps):
    tokens, width = hidden.shape
    experts = wr_t.shape[0]
    local, _, ffn = w1.shape
    slots = caps[-1] // local
    ft = ffn // NF
    vmem = pl.BlockSpec(memory_space=pltpu.VMEM)
    hbm = pl.BlockSpec(memory_space=pl.ANY)
    return pl.pallas_call(
        functools.partial(gather_kernel, caps),
        name='gather_tokens',
        out_shape=(
            pltpu.VMEM((local, owners, slots, width), BF16),
            jax.ShapeDtypeStruct((local * owners, tokens), F32),
            jax.ShapeDtypeStruct((tokens, 128), F32),
            jax.ShapeDtypeStruct((1,), I32),
            pltpu.VMEM((NF, width, ft), BF16),
            pltpu.VMEM((NF, width, ft), BF16),
            pltpu.VMEM((NF, ft, width), BF16),
        ),
        in_specs=[vmem, vmem, vmem, hbm, hbm, hbm],
        out_specs=(vmem, vmem, vmem, pl.BlockSpec(memory_space=pltpu.SMEM), vmem, vmem, vmem),
        scratch_shapes=[
            pltpu.VMEM((owners, tokens, width), BF16),
            pltpu.VMEM((owners, 2, tokens), I32),
            pltpu.SemaphoreType.DMA((25,)),
            pltpu.SemaphoreType.DMA((25,)),
            pltpu.SemaphoreType.DMA((owners,)),
            pltpu.SemaphoreType.DMA((owners,)),
            pltpu.SemaphoreType.DMA((NF, 3)),
        ],
        compiler_params=pltpu.CompilerParams(collective_id=0, has_side_effects=True, vmem_limit_bytes=20 * 1024 * 1024),
    )(hidden, ids_t, wr_t, w1, w3, w2)


def expert_kernel(caps, branch, pos, rows, w1p, w3p, w2p, w1, w3, w2, ret, w1b, w3b, w2b, mid, yacc, plan, wsem):
    local, owners, slots, width = rows.shape
    ft = w1b.shape[2]
    steps = (local - 1) * NF

    unit = []
    for j in range(local):
        most = jnp.max(pos[pl.ds(j * owners, owners), :]).astype(I32) + 1
        unit.append((most + 15) // 16)
    for j in range(local):
        rank = jnp.int32(min(j, 1))
        offset = jnp.int32(0)
        for i in range(local):
            if i > 0 and j > 0 and i != j:
                ahead = (unit[i] >= unit[j]) if i < j else (unit[i] > unit[j])
                rank = rank + ahead.astype(I32)
            if i < j:
                offset = offset + unit[i]
        plan[0, rank] = jnp.int32(j)
        plan[1, rank] = unit[j]
        plan[2, rank] = offset
    used = unit[0]
    for j in range(1, local):
        used = used + unit[j]

    def weights(t):
        e = plan[0, 1 + t // NF]
        cols = pl.ds(pl.multiple_of((t % NF) * ft, ft), ft)
        n = t % RING
        return (
            pltpu.make_async_copy(w1.at[e, :, cols], w1b.at[n], wsem.at[n, 0]),
            pltpu.make_async_copy(w3.at[e, :, cols], w3b.at[n], wsem.at[n, 1]),
            pltpu.make_async_copy(w2.at[e, cols, :], w2b.at[n], wsem.at[n, 2]),
        )

    for t in range(RING):
        for c in weights(jnp.int32(t)):
            c.start()

    limit = jnp.int32(caps[0])
    for n in range(1, len(caps)):
        limit = jnp.where(branch[0] >= n, caps[n], limit)

    @pl.loop(used, limit // 16)
    def _(n):
        blank = pl.ds(pl.multiple_of(n * 16, 16), 16)
        for q in range(owners):
            ret[q, blank, :] = jnp.zeros((16, width), BF16)

    def step(r, f, gate_w, up_w, down_w):
        e = plan[0, r]
        for units in range(1, slots // 16 + 1):
            m = 16 * units * owners

            @pl.when(plan[1, r] == units)
            def _():
                @pl.loop(0, ft // 256)
                def _(i):
                    cols = pl.ds(pl.multiple_of(i * 256, 256), 256)
                    x = rows[e, :, 0:16 * units, :].reshape(m, width)
                    gate = jnp.dot(x, gate_w[:, cols], preferred_element_type=F32)
                    up = jnp.dot(x, up_w[:, cols], preferred_element_type=F32)
                    mid[0:m, cols] = (gate * jax.nn.sigmoid(gate) * up).astype(BF16)

                @pl.loop(0, width // 512)
                def _(i):
                    cols = pl.ds(pl.multiple_of(i * 512, 512), 512)
                    part = jnp.dot(mid[0:m, :], down_w[:, cols], preferred_element_type=F32)
                    yacc[0:m, cols] = jnp.where(f == 0, 0.0, yacc[0:m, cols]) + part

                @pl.when(f == NF - 1)
                def _():
                    first = pl.multiple_of(plan[2, r] * 16, 16)
                    for q in range(owners):
                        ret[q, pl.ds(first, 16 * units), :] = yacc[q * 16 * units:(q + 1) * 16 * units, :].astype(BF16)

    @pl.loop(0, NF)
    def _(f):
        step(0, f, w1p.at[f], w3p.at[f], w2p.at[f])

    @pl.loop(0, steps)
    def _(t):
        n = t % RING
        for c in weights(t):
            c.wait()
        step(1 + t // NF, t % NF, w1b.at[n], w3b.at[n], w2b.at[n])

        @pl.when(t + RING < steps)
        def _():
            for c in weights(t + RING):
                c.start()


def expert_call(branch, pos, rows, w1p, w3p, w2p, w1, w3, w2, caps):
    local, owners, slots, width = rows.shape
    ft = w1p.shape[2]
    hbm = pl.BlockSpec(memory_space=pl.ANY)
    vmem = pl.BlockSpec(memory_space=pltpu.VMEM)
    flops = 3 * 2 * local * slots * owners * width * ft * NF // 2
    return pl.pallas_call(
        functools.partial(expert_kernel, caps),
        name='experts',
        out_shape=pltpu.VMEM((owners, caps[-1], width), BF16),
        in_specs=[pl.BlockSpec(memory_space=pltpu.SMEM), vmem, vmem, vmem, vmem, vmem, hbm, hbm, hbm],
        out_specs=vmem,
        scratch_shapes=[
            pltpu.VMEM((RING, width, ft), BF16),
            pltpu.VMEM((RING, width, ft), BF16),
            pltpu.VMEM((RING, ft, width), BF16),
            pltpu.VMEM((owners * slots, ft), BF16),
            pltpu.VMEM((owners * slots, width), F32),
            pltpu.SMEM((3, local), I32),
            pltpu.SemaphoreType.DMA((RING, 3)),
        ],
        compiler_params=pltpu.CompilerParams(vmem_limit_bytes=20 * 1024 * 1024),
        cost_estimate=pl.CostEstimate(flops=flops, bytes_accessed=3 * 2 * local * width * ft * NF, transcendentals=0),
    )(branch, pos, rows, w1p, w3p, w2p, w1, w3, w2)


ORDER = (0, 1, 2, 4, 6, 3, 5, 7)


def return_kernel(cap, ret, tok, hid, scale, out, got, acc, send, recv):
    me = lax.axis_index('ep')
    owners = ret.shape[0]
    tokens, width = hid.shape
    barrier = pltpu.get_barrier_semaphore()
    for q in range(1, owners):
        pl.semaphore_signal(barrier, inc=1, device_id=dev(flip(me, q)), device_id_type=MESH)
    pl.semaphore_wait(barrier, owners - 1)
    copies = {}
    for q in ORDER[2:] + (1,):
        copies[q] = pltpu.make_async_remote_copy(src_ref=ret.at[q, pl.ds(0, cap)], dst_ref=got.at[q], send_sem=send.at[q], recv_sem=recv.at[q], device_id=dev(flip(me, q)), device_id_type=MESH)
        copies[q].start()
    table = tok[...]
    lane = iota((tokens, cap), 1).astype(F32)
    for q in ORDER:
        if q != 0:
            copies[q].wait_recv()
        peer = flip(me, q).astype(F32)
        hot = jnp.concatenate([((table[:, 2 + k:3 + k] == peer) & (table[:, 4 + k:5 + k] == lane)).astype(F32) for k in (0, 1)], axis=0).astype(BF16)

        @pl.loop(0, width // 256)
        def _(n):
            cols = pl.ds(pl.multiple_of(n * 256, 256), 256)
            block = ret[0, 0:cap, cols] if q == 0 else got[q, :, cols]
            part = jnp.dot(hot, block, preferred_element_type=F32)
            acc[:, cols] = part if q == 0 else acc[:, cols] + part

    mixed = table[:, 0:1] * acc[0:tokens] + table[:, 1:2] * acc[tokens:2 * tokens]
    out[...] = (scale[0] * hid[...].astype(F32) + scale[1] * mixed).astype(BF16)
    for q in copies:
        copies[q].wait_send()


def return_call(n, cap, ret, tok, hidden, scale):
    owners, _, width = ret.shape
    tokens = hidden.shape[0]
    vmem = pl.BlockSpec(memory_space=pltpu.VMEM)
    return pl.pallas_call(
        functools.partial(return_kernel, cap),
        name=f'return_{cap}',
        out_shape=jax.ShapeDtypeStruct((tokens, width), BF16),
        in_specs=[vmem, vmem, vmem, pl.BlockSpec(memory_space=pltpu.SMEM)],
        out_specs=vmem,
        scratch_shapes=[
            pltpu.VMEM((owners, cap, width), BF16),
            pltpu.VMEM((2 * tokens, width), F32),
            pltpu.SemaphoreType.DMA((owners,)),
            pltpu.SemaphoreType.DMA((owners,)),
        ],
        compiler_params=pltpu.CompilerParams(collective_id=1 + n, has_side_effects=True, vmem_limit_bytes=24 * 1024 * 1024),
    )(ret, tok, hidden, scale)


def capacities(local, slots):
    full = [slots * n + 16 * (local - n) for n in range(1, local + 1)]
    return tuple(sorted({full[0] + 16, *full}))


def solution(mesh):
    owners = mesh.shape['ep']

    def local_step(hidden, router_w, expert_ids, w_gate, w_up, w_down, post_scale):
        tokens = hidden.shape[0]
        local = w_gate.shape[0]
        slots = tokens // max(1, local * owners // 8)
        caps = capacities(local, slots)
        rows, pos, tok, branch, w1p, w3p, w2p = gather_call(hidden, expert_ids.T, router_w.T, w_gate, w_up, w_down, owners, caps)
        ret = expert_call(branch, pos, rows, w1p, w3p, w2p, w_gate, w_up, w_down, caps)
        branches = [functools.partial(return_call, n, cap) for n, cap in enumerate(caps)]
        return lax.switch(branch[0], branches, ret, tok, hidden, post_scale)

    tok_spec = P(('dp', 'ep'))
    return jax.shard_map(local_step, mesh=mesh, in_specs=(tok_spec, P(), tok_spec, P('ep'), P('ep'), P('ep'), P()), out_specs=tok_spec, check_vma=False)
```

time: 140 us -> 112 us (0.80)
  Pallas kernels: 138 us -> 108 us
  local copies, waits for them, and re-layouts: 0.89 us -> 2.5 us
    pallas_call x1, Pallas kernels: 63.3 us -> 36 us  [return_call(): pl.pallas_call(functools.partial(return_kernel, cap), name=f'return_{cap}...]
    pallas_call x1, Pallas kernels: 39.4 us -> 37 us  [expert_call(): pl.pallas_call(functools.partial(expert_kernel, caps), name='experts', ou...]
    unnamed x5 -> x9, local copies, waits for them, and re-layouts: 0.89 us -> 2.5 us
where the time goes in v2:
time: 112 us
  Pallas kernels  108 us (96%)
  local copies, waits for them, and re-layouts  2.5 us (2%)
    pallas_call x1, Pallas kernels, expert_call(): pl.pallas_call(functools.partial(expert_kernel, caps), name='experts', ou...  37 us
    pallas_call x1, Pallas kernels, return_call(): pl.pallas_call(functools.partial(return_kernel, cap), name=f'return_{cap}...  36 us
    pallas_call x1, Pallas kernels, gather_call(): pl.pallas_call(functools.partial(gather_kernel, caps), name='gather_token...  35.2 us
    unnamed x9, local copies, waits for them, and re-layouts  2.5 us

profile of v2, /device:TPU:0, one launch (start us, length us, event | category | flops | bytes accessed | tf_op | source)
XLA Modules:
  0.0 111.6 jit_solution(722677716069464198)
XLA Ops:
  0.0 0.0 copy-start
  0.0 0.9 copy-done
  0.9 0.0 copy-start.1
  0.9 0.7 copy-done.1
  1.6 35.2 %gather_tokens.1 = (bf16[4,8,64,1536]{3,2,1,0:T(8,128)(2,1)S(1)}, f32[32,256]{1,0:T(8,128)S(1)}, f32[256,128]{1,0:T(8,128)S(1)}, s32[1]{0:T(128)}, bf16[3,1536,7...) custom-call(bf16[256,1536]{1,0:T(8,128)(2,1)} %hid.1, ...), custom_call_target="tpu_custom_call" | custom-call | tf_op jit(solution)/shard_map/gather_tokens/pallas_call | solution.py:194
  36.8 0.0 copy-start.2
  36.8 0.0 copy-start.3
  36.8 37.0 %experts.1 = bf16[8,256,1536]{2,1,0:T(8,128)(2,1)S(1)} custom-call(s32[1]{0:T(128)} %get-tuple-element.78.branch, f32[32,256]{1,0:T(8,128)S(1)} %get-tuple-element.79.pos, bf16[4,8,64,1536]{3,2,1,0:T(8,128)(2,1)S(1)} %get-tuple-element.80.rows, bf16[3,1536,768]{2,1,0:T(8,128)(2,1)S(1)} %get-tuple-element.81.w1p, ...), custom_call_target="tpu_custom_call" | custom-call | flops 21743271936 | bytes 84934656 | tf_op jit(solution)/shard_map/experts/pallas_call | solution.py:320
  74.5 0.0 copy-done.2
  74.5 0.0 copy-done.3
  74.5 36.2 %conditional.1 = (bf16[256,1536]{1,0:T(8,128)(2,1)S(1)}) conditional(s32[]{:T(128)} %bitcast.2, (bf16[8,256,1536]{2,1,0:T(8,128)(2,1)S(1)}, f32[256,128]{1,0:T(8,128)S(1)}, bf16[256,1536]{1,0:T(8,128)(2,1)S(1)}, f32[2]{0:T(128)S(1)}) %tuple.36, (bf16[8,256,1536]{2,1,0:T(8,128)(2,1)S(1)}, f32[256,128]{1,0:T(8,128)S(1)}, ...), branch_computations={%region_0.0_spmd, %region_1.0_spmd, %region_2.0_spmd, %region_3.0_... | conditional | bytes 8 | solution.py:412
  74.5 36.0 %return_112.1 = bf16[256,1536]{1,0:T(8,128)(2,1)S(1)} custom-call(bf16[8,256,1536]{2,1,0:T(8,128)(2,1)S(1)} %get-tuple-element.44.ret, f32[256,128]{1,0:T(8,128)S(1)} %get-tuple-element.50.tok, bf16[256,1536]{1,0:T(8,128)(2,1)S(1)} %get-tuple-element.52.hid, f32[2]{0:T(128)S(1)} %get-tuple-element.91.scale), custom_call_target="tpu_custom_call" | custom-call | tf_op jit(solution)/shard_map/cond/branch_0_fun/return_112/pallas_call | solution.py:380
  110.7 0.9 copy.24
Async XLA Ops:
  0.0 0.9 copy-start
  0.9 0.7 copy-start.1
  36.8 37.7 %copy-start.2 = (bf16[256,1536]{1,0:T(8,128)(2,1)S(1)}, bf16[256,1536]{1,0:T(8,128)(2,1)}, u32[]{:S(2)}) copy-start(bf16[256,1536]{1,0:T(8,128)(2,1)} %hid.1) | copy-start | bytes 2359300
  36.8 37.7 %copy-start.3 = (f32[2]{0:T(128)S(1)}, f32[2]{0:T(128)}, u32[]{:S(2)}) copy-start(f32[2]{0:T(128)} %param.18) | copy-start | bytes 28
